TPU v7x, 256 devices: a whole 4x4x8 slice. The times are simulated.
256 devices in a mesh: kpt: 128 (over x, z, y_hi, core), band: 2 (over y_lo).
Axes of the slice: x: 4, y: 4 (y_hi: 2, y_lo: 2; y = y_hi * 2 + y_lo), z: 8, core: 2. Of those that a mesh axis runs over, the one named last changes fastest.
Arguments:
- margins: bfloat16 [128, 12, 400, 800], P('kpt', None, 'band'), may hold values from -0.21875 to 0.21875
- subspace: bfloat16 [128, 400, 512], P('kpt', 'band'), may hold values from -6 to 6
- shell_weights: float32 [12], replicated, may hold values from 0.3 to 3
- window_count: int32 [128], P('kpt'), may hold values from 200 to 400
Outputs:
- new_subspace: float32 [128, 400, 512], P('kpt', 'band')
Inputs may be any that keep to these rules, and one draw needn't show every extreme that they name: window_count[k] is the number of leading bands of k-point k inside its outer window; the other rows up to 400 are padding.
All inputs are finite; a program needn't handle non-finite values.
Results may differ from a plain program's by a relative error of at most 0.0025.
Values may be sent and summed in bfloat16 or wider, within the bound.
A program may use at most 64 MiB of HBM per device.

v0:
```python
import math

import jax
import jax.numpy as jnp
from jax import lax
from jax.sharding import PartitionSpec as P

SWEEPS = 2


def from_behind(value, axis, steps):
    count = lax.axis_size(axis)
    pairs = [(source, (source + steps) % count) for source in range(count)]
    return lax.ppermute(value, axis, pairs)


def rows_first(arrays, axis, dims):
    turned = [jnp.moveaxis(a, dim, 0) for a, dim in zip(arrays, dims)]
    widths = [t[0].size for t in turned]
    both = jnp.concatenate([t.reshape(-1, w) for t, w in zip(turned, widths)], axis=1)
    out = lax.all_gather(both, axis, axis=0, tiled=True)
    tiles = jnp.split(out, [sum(widths[:k]) for k in range(1, len(widths))], axis=1)
    return tuple(
        (
            jnp.moveaxis(b.reshape(-1, *t.shape[1:]), 0, dim)
            for b, t, dim in zip(tiles, turned, dims)
        )
    )


def copy_for_each(shard, axis):
    copies = jnp.broadcast_to(shard, (lax.axis_size(axis), *shard.shape))
    return lax.all_to_all(copies, axis, split_axis=0, concat_axis=0, tiled=True)


def of_everyone(shard, axis):
    return copy_for_each(shard, axis).sum(axis=0)


def taken_together(shard, axis):
    everything = copy_for_each(shard, axis)
    return jnp.sum(everything.astype(jnp.float32), axis=0)


def grid_shape(point_count):
    size_y = min(4, point_count // 8)
    return (4, size_y, point_count // (4 * size_y))


def grid_place(point_index, point_count):
    size_x, size_y, size_z = grid_shape(point_count)
    return (point_index // (size_y * size_z), point_index // size_z % size_y, point_index % size_z)


def axis_neighbour(payload, direction, step, point_index, point_count, shifter):
    shape = grid_shape(point_count)
    strides = (shape[1] * shape[2], shape[2], 1)
    place = grid_place(point_index, point_count)
    stride = strides[direction]
    offset = step * stride
    inside = shifter(payload, -offset % point_count)
    if shape[direction] * stride == point_count:
        return inside
    wrapped = shifter(payload, -(offset - step * shape[direction] * stride) % point_count)
    coord = place[direction]
    outside = (coord + step < 0) | (coord + step >= shape[direction])
    return jnp.where(outside, wrapped, inside)


def sectioned_blocks(matrix, point_index, point_count, third_shift, second_shift, first_shift):
    third_up = axis_neighbour(matrix[None], 2, 1, point_index, point_count, third_shift)[0]
    third_down = axis_neighbour(matrix[None], 2, -1, point_index, point_count, third_shift)[0]
    trio = jnp.stack([matrix, third_up, third_down])
    second_up = axis_neighbour(trio, 1, 1, point_index, point_count, second_shift)
    second_down = axis_neighbour(trio, 1, -1, point_index, point_count, second_shift)
    quartet = jnp.stack([second_up[0], second_down[0], third_up, third_down])
    first_up = axis_neighbour(quartet, 0, 1, point_index, point_count, first_shift)
    first_down = axis_neighbour(quartet, 0, -1, point_index, point_count, first_shift)
    return jnp.stack(
        [
            first_up[0],
            first_up[1],
            first_down[0],
            first_down[1],
            first_up[2],
            first_up[3],
            first_down[2],
            first_down[3],
            second_up[1],
            second_up[2],
            second_down[1],
            second_down[2],
        ]
    )


def stack_complex(matrix, half_cols):
    real_part = matrix[..., :half_cols]
    imag_part = matrix[..., half_cols:]
    upper_half = jnp.concatenate([real_part, imag_part], axis=-1)
    lower_half = jnp.concatenate([-imag_part, real_part], axis=-1)
    return jnp.concatenate([upper_half, lower_half], axis=-2)


def gram_parts(iterate, half_cols):
    blocks = jnp.dot(iterate.T, iterate, precision=lax.Precision.HIGHEST)
    real_part = blocks[:half_cols, :half_cols] + blocks[half_cols:, half_cols:]
    imag_part = blocks[:half_cols, half_cols:] - blocks[half_cols:, :half_cols]
    return jnp.concatenate([real_part, imag_part], axis=1)


def sweep_step(iterate, gram_sum, half_cols):
    identity = jnp.eye(half_cols, dtype=jnp.float32)
    factor = jnp.concatenate(
        [1.5 * identity - 0.5 * gram_sum[:, :half_cols], -0.5 * gram_sum[:, half_cols:]], axis=1
    )
    return jnp.dot(iterate, stack_complex(factor, half_cols), precision=lax.Precision.HIGHEST)


def assemble(mine, whole, weights, half_cols):
    real_part = mine[..., :half_cols]
    imag_part = mine[..., half_cols:]
    left_rows = jnp.concatenate([mine, jnp.concatenate([imag_part, -real_part], axis=-1)], axis=-2)
    products = jnp.einsum("brc,bsc->brs", left_rows, whole, preferred_element_type=jnp.float32)
    summed = jnp.einsum("b,brs->rs", weights, products, precision=lax.Precision.HIGHEST)
    row_count = mine.shape[-2]
    return jnp.concatenate([summed[:row_count], summed[row_count:]], axis=1)


def on_device(margins, subspace, shell_weights, window_count):
    half_cols = subspace.shape[-1] // 2
    row_count = subspace.shape[1]
    point_count = lax.axis_size("kpt")
    point_index = lax.axis_index("kpt")
    own_block = subspace[0]
    row_index = lax.axis_index("band") * row_count + lax.iota(jnp.int32, row_count)
    row_mask = (row_index < window_count[0])[None, :, None]
    nearby = sectioned_blocks(
        own_block,
        point_index,
        point_count,
        lambda payload, amount: from_behind(payload, "kpt", amount),
        lambda payload, amount: from_behind(payload, "kpt", amount),
        lambda payload, amount: from_behind(payload, "kpt", amount),
    )
    nearby_whole, own_whole = rows_first((nearby, own_block), "band", (1, 0))
    products = jnp.einsum(
        "brc,bcs->brs",
        margins[0],
        stack_complex(nearby_whole, half_cols),
        preferred_element_type=jnp.float32,
    )
    projected = jnp.where(row_mask, products, 0.0).astype(jnp.bfloat16)
    projected_whole = lax.all_gather(projected, "band", axis=1, tiled=True)
    assembled = assemble(projected, projected_whole, shell_weights, half_cols)
    iterate = jnp.dot(
        assembled,
        stack_complex(own_whole.astype(jnp.float32), half_cols),
        precision=lax.Precision.HIGHEST,
    )
    gram_sum = of_everyone(gram_parts(iterate, half_cols), "band")
    squares = jnp.trace(gram_sum[:, :half_cols])
    scaling = lax.rsqrt(2.0 * squares / half_cols + 1e-06)
    iterate = iterate * scaling
    gram_sum = gram_sum * (scaling * scaling)
    for sweep_number in range(SWEEPS):
        if sweep_number > 0:
            gram_sum = taken_together(
                gram_parts(iterate, half_cols).astype(jnp.bfloat16), "band"
            ).astype(jnp.float32)
        iterate = sweep_step(iterate, gram_sum, half_cols)
    return (iterate * math.sqrt(row_count * lax.axis_size("band")))[None]


def solution(mesh):
    return jax.shard_map(
        on_device,
        mesh=mesh,
        in_specs=(P("kpt", None, "band", None), P("kpt", "band", None), P(), P("kpt")),
        out_specs=P("kpt", "band", None),
        check_vma=False,
    )
```

profile of v0, /device:TPU:8, one launch (start us, length us, event | category | flops | bytes accessed | tf_op | source)
XLA Modules:
  0.0 347.2 jit_solution(3580475012006740323)
XLA Ops:
  6.5 10.5 %collective-permute-start.2 = (bf16[1,200,512]{2,1,0:T(8,128)(2,1)}, bf16[1,200,512]{2,1,0:T(8,128)(2,1)S(1)}, u32[]{:S(2)}, u32[]{:S(2)}) collective-permute-start(bf16[1,200,512]{2,1,0:T(8,128)(2,1)} %param.5), channel_id=1, source_target_pairs={{0,242},{2,244},{4,246},{6,248},{8,250},{10,252},{12,254},{14,0},{... | collective-permute-start | bytes 614408 | tf_op jit(solution)/shard_map/ppermute | solution.py:14
  17.7 1.7 collective-permute-done.3
  19.4 7.0 %collective-permute-done.2 = bf16[1,200,512]{2,1,0:T(8,128)(2,1)S(1)} collective-permute-done((bf16[1,200,512]{2,1,0:T(8,128)(2,1)}, bf16[1,200,512]{2,1,0:T(8,128)(2,1)S(1)}, u32[]{:S(2)}, u32[]{:S(2)}) %collective-permute-start.2) | collective-permute-done | bytes 204832 | tf_op jit(solution)/shard_map/ppermute | solution.py:14
  26.4 2.2 collective-permute-done.1
  29.1 1.0 pad_maximum_fusion.2
  30.2 2.6 collective-permute-start.6
  32.8 3.7 %collective-permute-start.5 = (bf16[3,200,512]{2,1,0:T(8,128)(2,1)S(1)}, bf16[3,200,512]{2,1,0:T(8,128)(2,1)S(1)}, u32[]{:S(2)}, u32[]{:S(2)}) collective-permute-start(bf16[3,200,512]{2,1,0:T(8,128)(2,1)S(1)} %pad_maximum_fusion.2), channel_id=1, source_target_pairs={{0,240},{2,242},{4,244},{6,246},{8,248},{10,250},{12,252},{14,254}... | collective-permute-start | bytes 1843208 | tf_op jit(solution)/shard_map/ppermute | solution.py:14
  36.4 2.9 collective-permute-start.4
  39.4 7.0 %collective-permute-done.7 = bf16[3,200,512]{2,1,0:T(8,128)(2,1)S(1)} collective-permute-done((bf16[3,200,512]{2,1,0:T(8,128)(2,1)S(1)}, bf16[3,200,512]{2,1,0:T(8,128)(2,1)S(1)}, u32[]{:S(2)}, u32[]{:S(2)}) %collective-permute-start.7) | collective-permute-done | bytes 614432 | tf_op jit(solution)/shard_map/ppermute | solution.py:14
  46.3 19.5 %collective-permute-done.6 = bf16[3,200,512]{2,1,0:T(8,128)(2,1)S(1)} collective-permute-done((bf16[3,200,512]{2,1,0:T(8,128)(2,1)S(1)}, bf16[3,200,512]{2,1,0:T(8,128)(2,1)S(1)}, u32[]{:S(2)}, u32[]{:S(2)}) %collective-permute-start.6) | collective-permute-done | bytes 614432 | tf_op jit(solution)/shard_map/ppermute | solution.py:14
  65.9 11.3 %collective-permute-done.4 = bf16[3,200,512]{2,1,0:T(8,128)(2,1)S(1)} collective-permute-done((bf16[3,200,512]{2,1,0:T(8,128)(2,1)S(1)}, bf16[3,200,512]{2,1,0:T(8,128)(2,1)S(1)}, u32[]{:S(2)}, u32[]{:S(2)}) %collective-permute-start.4) | collective-permute-done | bytes 614432 | tf_op jit(solution)/shard_map/ppermute | solution.py:14
  77.5 0.9 collective-permute-start.8
  78.4 1.2 collective-permute-start.9
  79.6 10.3 %collective-permute-done.8 = bf16[4,200,512]{2,1,0:T(8,128)(2,1)S(1)} collective-permute-done((bf16[4,200,512]{2,1,0:T(8,128)(2,1)S(1)}, bf16[4,200,512]{2,1,0:T(8,128)(2,1)S(1)}, u32[]{:S(2)}, u32[]{:S(2)}) %collective-permute-start.8) | collective-permute-done | bytes 819232 | tf_op jit(solution)/shard_map/ppermute | solution.py:14
  89.9 2.0 collective-permute-done.9
  93.0 1.7 pad_maximum_fusion
  95.7 93.8 %all-gather.3.cloned.1.call-done = bf16[400,6656]{1,0:T(8,128)(2,1)} async-done(((bf16[200,6656]{1,0:T(8,128)(2,1)}), bf16[400,6656]{1,0:T(8,128)(2,1)}) %all-gather.3.cloned.1.call-update) | async-done | bytes 5324816 | tf_op jit(solution)/shard_map/all_gather | solution.py:21
  189.4 2.4 slice-done
  192.6 5.6 %fusion.15 = bf16[12,200,512]{2,1,0:T(8,128)(2,1)} fusion(pred[200]{0:T(512)(128)(4,1)S(1)} %add_compare_fusion, bf16[1,12,200,800]{3,2,1,0:T(8,128)(2,1)} %param.4, bf16[12,400,256]{2,1,0:T(8,128)(2,1)S(1)} %get-tuple-element.6, bf16[12,400,256]{2,1,0:T(8,128)(2,1)S(1)} %get-tuple-element.5, bf16[12,400,512]{2,1,0:T(8,128)(2,1)S(1)} %bitcast.35), kind=kOutput, calls=%fused_computation.18 | convolution fusion | flops 1998028800 | bytes 16128200 | tf_op jit(solution)/shard_map/brc,bcs->brs/dot_general | solution.py:147
  198.2 1.2 slice_convert_fusion
  199.5 1.0 slice_negate_fusion.2
  200.4 1.6 fusion.58
  202.0 67.3 %all-gather.5.cloned.1.call-done = bf16[12,400,512]{2,1,0:T(8,128)(2,1)} async-done(((bf16[12,200,512]{2,1,0:T(8,128)(2,1)}), bf16[12,400,512]{2,1,0:T(8,128)(2,1)}) %all-gather.5.cloned.1.call-update) | async-done | bytes 4915216 | tf_op jit(solution)/shard_map/all_gather | solution.py:154
  269.3 9.6 %fusion.8 = f32[12,400,400]{2,1,0:T(8,128)} fusion(bf16[12,400,512]{2,1,0:T(8,128)(2,1)} %all-gather.5.cloned.1.call-done, bf16[12,200,256]{2,1,0:T(8,128)(2,1)} %get-tuple-element.8, bf16[12,200,256]{2,1,0:T(8,128)(2,1)} %get-tuple-element.7, bf16[12,200,512]{2,1,0:T(8,128)(2,1)S(1)} %copy-done.1), kind=kOutput, calls=%fused_computation.9 | convolution fusion | flops 1980825600 | bytes 17510400 | tf_op jit(solution)/shard_map/brc,bsc->brs/dot_general | solution.py:124
  279.0 25.7 %fusion = f32[1,400,400]{2,0,1:T(1,128)S(1)} fusion(f32[12,400,400]{2,1,0:T(8,128)} %fusion.8, f32[12]{0:T(128)S(1)} %copy-done), kind=kOutput, calls=%fused_computation | convolution fusion | flops 23040000 | bytes 8320048 | tf_op jit(solution)/shard_map/b,brs->rs/dot_general | solution.py:125
  305.8 1.6 fusion.16
  307.4 1.1 fusion.60
  309.0 16.1 %all_to_all.10 = f32[2,256,512]{2,1,0:T(8,128)S(1)} all-to-all(f32[2,256,512]{2,1,0:T(8,128)S(1)} %broadcast_in_dim.28), channel_id=1, replica_groups=mesh['kpt'=128,'band'=2] {'band'}, dimensions={0} | all-to-all | bytes 2097152 | tf_op jit(solution)/shard_map/all_to_all | solution.py:33
  326.7 0.9 fusion.27
  327.6 1.1 fusion.61
  329.0 9.6 %all_to_all.11 = bf16[2,256,512]{2,1,0:T(8,128)(2,1)S(1)} all-to-all(bf16[2,256,512]{2,1,0:T(8,128)(2,1)S(1)} %broadcast_in_dim.30), channel_id=1, replica_groups=mesh['kpt'=128,'band'=2] {'band'}, dimensions={0} | all-to-all | bytes 1048576 | tf_op jit(solution)/shard_map/all_to_all | solution.py:33
  338.8 1.6 fusion.26
  (54 shorter events, 6.5 us)
Async XLA Ops:
  6.5 272.4 %copy-start = (f32[12]{0:T(128)S(1)}, f32[12]{0:T(128)}, u32[]{:S(2)}) copy-start(f32[12]{0:T(128)} %param.6) | copy-start | bytes 148
  6.5 182.9 %all-gather.3.cloned.1.call-start = ((), (), s32[]{:S(2)}) async-start(), calls=%async_computation.2 | async-start | bytes 7987200 | tf_op jit(solution)/shard_map/all_gather | solution.py:21
  6.5 12.9 %collective-permute-start.3 = (bf16[1,200,512]{2,1,0:T(8,128)(2,1)}, bf16[1,200,512]{2,1,0:T(8,128)(2,1)S(1)}, u32[]{:S(2)}, u32[]{:S(2)}) collective-permute-start(bf16[1,200,512]{2,1,0:T(8,128)(2,1)} %param.5), channel_id=1, source_target_pairs={{0,2},{2,4},{4,6},{6,8},{8,10},{10,12},{12,14},{14,16},{16,18},{18... | collective-permute-start | bytes 614408 | tf_op jit(solution)/shard_map/ppermute | solution.py:14
  6.5 19.8 %collective-permute-start.2 = (bf16[1,200,512]{2,1,0:T(8,128)(2,1)}, bf16[1,200,512]{2,1,0:T(8,128)(2,1)S(1)}, u32[]{:S(2)}, u32[]{:S(2)}) collective-permute-start(bf16[1,200,512]{2,1,0:T(8,128)(2,1)} %param.5), channel_id=1, source_target_pairs={{0,242},{2,244},{4,246},{6,248},{8,250},{10,252},{12,254},{14,0},{... | collective-permute-start | bytes 614408 | tf_op jit(solution)/shard_map/ppermute | solution.py:14
  17.1 11.5 %collective-permute-start.1 = (bf16[1,200,512]{2,1,0:T(8,128)(2,1)}, bf16[1,200,512]{2,1,0:T(8,128)(2,1)S(1)}, u32[]{:S(2)}, u32[]{:S(2)}) collective-permute-start(bf16[1,200,512]{2,1,0:T(8,128)(2,1)} %param.5), channel_id=1, source_target_pairs={{0,254},{2,0},{4,2},{6,4},{8,6},{10,8},{12,10},{14,12},{16,14},{18... | collective-permute-start | bytes 614408 | tf_op jit(solution)/shard_map/ppermute | solution.py:14
  17.7 11.3 %collective-permute-start = (bf16[1,200,512]{2,1,0:T(8,128)(2,1)}, bf16[1,200,512]{2,1,0:T(8,128)(2,1)S(1)}, u32[]{:S(2)}, u32[]{:S(2)}) collective-permute-start(bf16[1,200,512]{2,1,0:T(8,128)(2,1)} %param.5), channel_id=1, source_target_pairs={{0,14},{2,16},{4,18},{6,20},{8,22},{10,24},{12,26},{14,28},{16,30}... | collective-permute-start | bytes 614408 | tf_op jit(solution)/shard_map/ppermute | solution.py:14
  30.1 16.2 %collective-permute-start.7 = (bf16[3,200,512]{2,1,0:T(8,128)(2,1)S(1)}, bf16[3,200,512]{2,1,0:T(8,128)(2,1)S(1)}, u32[]{:S(2)}, u32[]{:S(2)}) collective-permute-start(bf16[3,200,512]{2,1,0:T(8,128)(2,1)S(1)} %pad_maximum_fusion.2), channel_id=1, source_target_pairs={{0,16},{2,18},{4,20},{6,22},{8,24},{10,26},{12,28},{14,30},{16,32}... | collective-permute-start | bytes 1843208 | tf_op jit(solution)/shard_map/ppermute | solution.py:14
  30.2 35.6 %collective-permute-start.6 = (bf16[3,200,512]{2,1,0:T(8,128)(2,1)S(1)}, bf16[3,200,512]{2,1,0:T(8,128)(2,1)S(1)}, u32[]{:S(2)}, u32[]{:S(2)}) collective-permute-start(bf16[3,200,512]{2,1,0:T(8,128)(2,1)S(1)} %pad_maximum_fusion.2), channel_id=1, source_target_pairs={{0,208},{2,210},{4,212},{6,214},{8,216},{10,218},{12,220},{14,222}... | collective-permute-start | bytes 1843208 | tf_op jit(solution)/shard_map/ppermute | solution.py:14
  32.8 33.1 %collective-permute-start.5 = (bf16[3,200,512]{2,1,0:T(8,128)(2,1)S(1)}, bf16[3,200,512]{2,1,0:T(8,128)(2,1)S(1)}, u32[]{:S(2)}, u32[]{:S(2)}) collective-permute-start(bf16[3,200,512]{2,1,0:T(8,128)(2,1)S(1)} %pad_maximum_fusion.2), channel_id=1, source_target_pairs={{0,240},{2,242},{4,244},{6,246},{8,248},{10,250},{12,252},{14,254}... | collective-permute-start | bytes 1843208 | tf_op jit(solution)/shard_map/ppermute | solution.py:14
  36.4 40.8 %collective-permute-start.4 = (bf16[3,200,512]{2,1,0:T(8,128)(2,1)S(1)}, bf16[3,200,512]{2,1,0:T(8,128)(2,1)S(1)}, u32[]{:S(2)}, u32[]{:S(2)}) collective-permute-start(bf16[3,200,512]{2,1,0:T(8,128)(2,1)S(1)} %pad_maximum_fusion.2), channel_id=1, source_target_pairs={{0,48},{2,50},{4,52},{6,54},{8,56},{10,58},{12,60},{14,62},{16,64}... | collective-permute-start | bytes 1843208 | tf_op jit(solution)/shard_map/ppermute | solution.py:14
  77.5 12.4 %collective-permute-start.8 = (bf16[4,200,512]{2,1,0:T(8,128)(2,1)S(1)}, bf16[4,200,512]{2,1,0:T(8,128)(2,1)S(1)}, u32[]{:S(2)}, u32[]{:S(2)}) collective-permute-start(bf16[4,200,512]{2,1,0:T(8,128)(2,1)S(1)} %pad_maximum_fusion.1), channel_id=1, source_target_pairs={{0,192},{2,194},{4,196},{6,198},{8,200},{10,202},{12,204},{14,206}... | collective-permute-start | bytes 2457608 | tf_op jit(solution)/shard_map/ppermute | solution.py:14
  78.4 13.6 %collective-permute-start.9 = (bf16[4,200,512]{2,1,0:T(8,128)(2,1)S(1)}, bf16[4,200,512]{2,1,0:T(8,128)(2,1)S(1)}, u32[]{:S(2)}, u32[]{:S(2)}) collective-permute-start(bf16[4,200,512]{2,1,0:T(8,128)(2,1)S(1)} %pad_maximum_fusion.1), channel_id=1, source_target_pairs={{0,64},{2,66},{4,68},{6,70},{8,72},{10,74},{12,76},{14,78},{16,80}... | collective-permute-start | bytes 2457608 | tf_op jit(solution)/shard_map/ppermute | solution.py:14
  92.1 0.9 copy-start.2
  94.8 174.5 %all-gather.5.cloned.1.call-start = ((), (), s32[]{:S(2)}) async-start(), calls=%async_computation.3 | async-start | bytes 7372800 | tf_op jit(solution)/shard_map/all_gather | solution.py:154
  189.4 2.4 slice-start
  198.2 2.2 copy-start.1
  304.7 1.0 copy-start.3
  304.7 1.1 copy-start.4
Sparse Core Ops, SparseCore 0:
  94.9 94.4 all-gather.2
  198.4 70.9 all-gather.4
where the time goes:
time: 349 us; the launch traced here: 347 us
  waiting for transfers between devices  223 us (64%)
  matrix products  47.3 us (14%)
  blocking collectives  25.8 us (7%)
  starting transfers between devices  22.8 us (7%)
  between operations  15.1 us (4%)
  other arithmetic  8.28 us (2%)
  local copies, waits for them, and re-layouts  5.6 us (2%)
    all_gather x1, waiting for transfers between devices, rows_first(): out = lax.all_gather(both, axis, axis=0, tiled=True)  93.8 us
    all_gather x1, waiting for transfers between devices, on_device(): projected_whole = lax.all_gather(projected, 'band', axis=1, tiled=True)  67.3 us
    ppermute x10, waiting for transfers between devices, from_behind(): return lax.ppermute(value, axis, pairs)  61.4 us
    all_to_all x2, blocking collectives, copy_for_each(): return lax.all_to_all(copies, axis, split_axis=0, concat_axis=0, tiled=True)  25.8 us
    dot_general x1, matrix products, assemble(): jnp.einsum('b,brs->rs', weights, products, precision=lax.Precision.HIGHEST)  25.7 us
    ppermute x10, starting transfers between devices, from_behind(): return lax.ppermute(value, axis, pairs)  22.5 us
    dot_general x1, matrix products, assemble(): jnp.einsum('brc,bsc->brs', left_rows, whole, preferred_element_type=jnp.f...  9.64 us
  transfers between devices with their start and end apart: 12, of which 11 were waited for; matrix products, arithmetic and copies ran while one was open for 1% of the time, Pallas kernels for 0%

commit v1 on v0

v1 whole, which is shorter than its diff:
```python
import functools
import math

import jax
import jax.numpy as jnp
from jax import lax
from jax.experimental import pallas as pl
from jax.experimental.pallas import tpu as pltpu
from jax.sharding import PartitionSpec as P

SIZE_X, SIZE_Y, SIZE_Z = 4, 4, 8
ROWS = 200
PAD = 208
DEEP = 256
COLS = 512
HALF = 256
SHELL = 12
MESH = pl.DeviceIdType.MESH
F32 = jnp.float32
BF16 = jnp.bfloat16


def dot(a, b):
    return jnp.dot(a, b, preferred_element_type=F32)


def dot_nt(a, b):
    return lax.dot_general(a, b, (((1,), (1,)), ((), ())), preferred_element_type=F32)


def dot_tn(a, b):
    return lax.dot_general(a, b, (((0,), (0,)), ((), ())), preferred_element_type=F32)


def halves(a):
    high = a.astype(BF16)
    return high, (a - high.astype(F32)).astype(BF16)


def dot3(a, b, product=dot):
    a_high, a_low = halves(a)
    b_high, b_low = halves(b)
    return product(a_high, b_high) + (product(a_high, b_low) + product(a_low, b_high))


def complex_rows(both, rows, start):
    upper, lower = both[:rows], both[start:start + rows]
    return jnp.concatenate(
        [upper[:, :HALF] - lower[:, HALF:], upper[:, HALF:] + lower[:, :HALF]], axis=1
    )


def stack_complex(real, imag):
    return jnp.concatenate(
        [jnp.concatenate([real, imag], axis=1), jnp.concatenate([-imag, real], axis=1)], axis=0
    )


def kernel(
    window_ref, weight_ref, margin_ref, own_ref, out_ref,
    raw, split, near, mine, rotated, theirs, diag, cross, packed, arrived,
    raw_sem, first_send, first_recv, block_send, block_recv, relay_send, proj_send, proj_recv, z_send, z_recv,
):
    kpt = lax.axis_index("kpt")
    band = lax.axis_index("band")
    other = 1 - band
    i = lax.div(kpt, SIZE_Y * SIZE_Z)
    j = lax.rem(lax.div(kpt, SIZE_Z), SIZE_Y)
    l = lax.rem(kpt, SIZE_Z)
    odd = lax.rem(l, 2)

    def point(di, dj, new_l):
        new_i = lax.rem(i + di + SIZE_X, SIZE_X)
        new_j = lax.rem(j + dj + SIZE_Y, SIZE_Y)
        return (new_i * SIZE_Y + new_j) * SIZE_Z + new_l

    l_near = l + 1 - 2 * odd
    l_far = lax.rem(l + 2 * odd - 1 + SIZE_Z, SIZE_Z)
    l_hop = lax.rem(l + 2 - 4 * odd + SIZE_Z, SIZE_Z)
    l_back = lax.rem(l - 2 + 4 * odd + SIZE_Z, SIZE_Z)

    steps = ((1, 0), (-1, 0), (0, 1), (0, -1))
    near_peers = [(point(-di, -dj, l_near), band) for di, dj in steps]
    far_peers = [(point(-di, -dj, l_far), other) for di, dj in steps]
    hop_peer = (point(0, 0, l_hop), other)
    back_peer = (point(0, 0, l_back), other)
    partner = (kpt, other)

    shell = [
        4 + odd, 6 + odd, 8 + odd, 10 + odd, 5 - odd, 7 - odd,
        0, 2, 1, 3, 9 - odd, 11 - odd,
    ]

    loads = [
        pltpu.make_async_copy(margin_ref.at[shell[s]], raw.at[s], raw_sem.at[s]) for s in range(SHELL)
    ]
    for load in loads:
        load.start()

    def clear(s, carry):
        near[s, ROWS:] = jnp.zeros((DEEP - ROWS, COLS), BF16)
        return carry

    lax.fori_loop(0, 2 * SHELL + 2, clear, 0)
    theirs[:, PAD:] = jnp.zeros((6, DEEP - PAD, COLS), BF16)

    barrier = pltpu.get_barrier_semaphore()
    peers = near_peers + far_peers[:2] + [hop_peer, back_peer, partner]
    for peer in peers:
        pl.semaphore_signal(barrier, inc=1, device_id=peer, device_id_type=MESH)
    pl.semaphore_wait(barrier, len(peers))

    def send(src, dst, send_sem, recv_sem, peer):
        copy = pltpu.make_async_remote_copy(
            src_ref=src, dst_ref=dst, send_sem=send_sem, recv_sem=recv_sem, device_id=peer, device_id_type=MESH
        )
        copy.start()
        return copy

    def block(s, q):
        return near.at[2 * s + q, pl.ds(0, ROWS)]

    def wait_block(s, q):
        pltpu.make_async_remote_copy(
            src_ref=block(s, q), dst_ref=block(s, q), send_sem=block_send.at[0, 0], recv_sem=block_recv.at[2 * s + q],
            device_id=partner, device_id_type=MESH,
        ).wait_recv()

    u_own = own_ref.at[0]
    u_other = near.at[2 * SHELL + 1, pl.ds(0, ROWS)]
    sent = []

    def direct(s, src, q, turn):
        peer = near_peers[s] if s < 4 else far_peers[s - 4]
        sent.append(send(src, block(s, q), block_send.at[s, turn], block_recv.at[2 * s + q], peer))

    first = send(u_own, u_other, first_send, first_recv, partner)
    for s in range(6):
        direct(s, u_own, band, 0)

    near[2 * SHELL, :ROWS] = own_ref[0]
    diag[...] = jnp.zeros_like(diag)
    cross[...] = jnp.zeros_like(cross)
    split[...] = jnp.zeros_like(split)
    for load in loads:
        load.wait()

    def separate(s, carry):
        whole = raw[s]
        for part in range(4):
            piece = whole[:, part * ROWS:(part + 1) * ROWS]
            split[2 * s + part % 2, (part // 2) * PAD:(part // 2) * PAD + ROWS, :ROWS] = piece
        return carry

    lax.fori_loop(0, 6, separate, 0)

    first.wait_recv()
    for s in range(6):
        direct(s, u_other, other, 1)

    lax.fori_loop(6, SHELL, separate, 0)

    def relays(s, q, turn):
        targets = {2: ((6, near_peers[0]), (7, near_peers[1]), (10, hop_peer)),
                   3: ((8, near_peers[0]), (9, near_peers[1]), (11, hop_peer))}[s]
        return [
            pltpu.make_async_remote_copy(
                src_ref=block(s, q), dst_ref=block(target, q), send_sem=relay_send.at[s, n, turn],
                recv_sem=block_recv.at[2 * target + q], device_id=peer, device_id_type=MESH,
            )
            for n, (target, peer) in enumerate(targets)
        ]

    def relay(s, q, turn):
        for copy in relays(s, q, turn):
            copy.start()

    row = lax.broadcasted_iota(jnp.int32, (PAD, 1), 0)
    inside = (row < ROWS) & (row + band * ROWS < window_ref[0])

    def project(s, carry):
        both = dot(split[2 * s], near[2 * s]) + dot(split[2 * s + 1], near[2 * s + 1])
        projected = jnp.where(inside, complex_rows(both, PAD, PAD), 0.0).astype(BF16)
        mine[s] = projected
        rotated[0:PAD] = projected
        rotated[PAD:, :HALF] = projected[:, HALF:]
        rotated[PAD:, HALF:] = -projected[:, :HALF]
        diag[...] += weight_ref[shell_of(s)] * dot_nt(rotated[...], projected)
        return carry

    def shell_of(s):
        near_b = 4 + 2 * s + odd
        far_x = 5 + 2 * (s - 4) - odd
        corner = 2 * lax.rem(s, 2) + lax.div(s - 6, 2)
        far_y = 9 + 2 * (s - 10) - odd
        return jnp.where(s < 4, near_b, jnp.where(s < 6, far_x, jnp.where(s < 10, corner, far_y)))

    def proj_copy(t):
        return pltpu.make_async_remote_copy(
            src_ref=mine.at[2 * t + band], dst_ref=theirs.at[t, pl.ds(0, PAD)],
            send_sem=proj_send.at[t], recv_sem=proj_recv.at[t], device_id=partner, device_id_type=MESH,
        )

    def meet(t):
        proj_copy(t).wait_recv()
        s = 2 * t + other
        projected = mine[s]
        rotated[0:PAD] = projected
        rotated[PAD:, :HALF] = projected[:, HALF:]
        rotated[PAD:, HALF:] = -projected[:, :HALF]
        cross[...] += weight_ref[shell_of(s)] * dot_nt(rotated[...], theirs[t])

    for s in (0, 1):
        wait_block(s, band)
    for s in (2, 3):
        wait_block(s, band)
        relay(s, band, 0)
    for s in (0, 1):
        wait_block(s, other)

    def pair(t, carry):
        @pl.when(t == 1)
        def _():
            for s in (2, 3):
                wait_block(s, other)
                relay(s, other, 1)

        @pl.when(t >= 2)
        def _():
            for u in range(2):
                for q in range(2):
                    wait_block(2 * t + u, q)

        lax.fori_loop(2 * t, 2 * t + 2, project, 0)
        proj_copy(t).start()

        @pl.when(t >= 1)
        def _():
            meet(t - 1)

        return carry

    lax.fori_loop(0, 6, pair, 0)
    meet(5)

    place_row = lax.broadcasted_iota(jnp.int32, (PAD, DEEP), 0)
    place_col = lax.broadcasted_iota(jnp.int32, (PAD, DEEP), 1)
    upper = place_row <= place_col
    packed[0] = cross[:PAD].astype(BF16)
    packed[1] = cross[PAD:].astype(BF16)
    packed[2, :, :PAD] = jnp.where(upper[:, :PAD], diag[:PAD], diag[PAD:]).astype(BF16)
    packed[2, :, PAD:] = jnp.zeros((PAD, DEEP - PAD), BF16)
    swap = send(packed, arrived, z_send, z_recv, partner)

    u_h = near[2 * SHELL]
    u_o = near[2 * SHELL + 1]
    diag_high, diag_low = halves(diag[...])
    cross_high, cross_low = halves(cross[...])
    x_h = (
        dot(diag_high, u_h[:PAD]) + dot(diag_low, u_h[:PAD]) + (dot(cross_high, u_o) + dot(cross_low, u_o))
    )
    flipped_high = jnp.concatenate([cross_high[:PAD], -cross_high[PAD:]], axis=1)
    flipped_low = jnp.concatenate([cross_low[:PAD], -cross_low[PAD:]], axis=1)
    x_o = dot_tn(flipped_high, u_h[:PAD]) + dot_tn(flipped_low, u_h[:PAD])

    swap.wait_recv()
    got = arrived[...]
    zero = jnp.zeros((PAD, DEEP), BF16)
    got_diag = got[2].astype(F32)
    got_real = jnp.where(upper, got_diag, 0.0).astype(BF16)
    got_above = jnp.where(place_row < place_col, got_diag, 0.0).astype(BF16)
    got_imag = jnp.where(upper, 0.0, got_diag).astype(BF16)
    x_h_late = dot_tn(jnp.concatenate([got[0], -got[1]], axis=1), u_o[:PAD])
    x_o_late = dot_tn(jnp.concatenate([got_above, -got_imag], axis=1), u_o[:PAD])
    x_o_plain = dot(jnp.concatenate([got_real, got_imag], axis=0), u_o) + dot(
        jnp.concatenate([got[0], got[1]], axis=0), u_h
    )
    x_h = complex_rows(x_h, PAD, PAD) + complex_rows(x_h_late, PAD, DEEP)
    x_o = complex_rows(x_o + x_o_late, PAD, DEEP) + complex_rows(x_o_plain, PAD, PAD)

    x_all = jnp.concatenate([x_h, x_o], axis=0)
    squares = jnp.sum(jnp.sum(x_all * x_all, axis=0, keepdims=True), axis=1, keepdims=True)
    scale = lax.rsqrt(2.0 * squares / HALF + 1e-06)
    gram = dot3(x_all, x_all, dot_tn) * (scale * scale)
    gram_real = gram[:HALF, :HALF] + gram[HALF:, HALF:]
    gram_imag = gram[:HALF, HALF:] - gram[HALF:, :HALF]
    eye = (
        lax.broadcasted_iota(jnp.int32, (HALF, HALF), 0) == lax.broadcasted_iota(jnp.int32, (HALF, HALF), 1)
    ).astype(F32)
    factor = stack_complex(1.5 * eye - 0.5 * gram_real, -0.5 * gram_imag)
    stacked = jnp.concatenate([x_h, jnp.concatenate([gram_real, gram_imag], axis=1)], axis=0)
    stacked = dot3(stacked, factor)
    gram = dot3(stacked[PAD:], factor)
    factor = stack_complex(1.5 * eye - 0.5 * gram[:, :HALF], -0.5 * gram[:, HALF:])
    out_ref[0] = (dot3(stacked[:PAD], factor) * (scale * math.sqrt(2.0 * ROWS)))[:ROWS]

    first.wait_send()
    for copy in sent:
        copy.wait_send()
    for s in (2, 3):
        for turn, q in enumerate((band, other)):
            for copy in relays(s, q, turn):
                copy.wait_send()
    for t in range(6):
        proj_copy(t).wait_send()
    swap.wait_send()


def on_device(margins, subspace, shell_weights, window_count):
    vmem = pl.BlockSpec(memory_space=pltpu.VMEM)
    smem = pl.BlockSpec(memory_space=pltpu.SMEM)
    return pl.pallas_call(
        kernel,
        out_shape=jax.ShapeDtypeStruct((1, ROWS, COLS), F32),
        in_specs=[smem, smem, pl.BlockSpec(memory_space=pl.ANY), vmem],
        out_specs=vmem,
        scratch_shapes=[
            pltpu.VMEM((SHELL, ROWS, 4 * ROWS), BF16),
            pltpu.VMEM((2 * SHELL, 2 * PAD, DEEP), BF16),
            pltpu.VMEM((2 * SHELL + 2, DEEP, COLS), BF16),
            pltpu.VMEM((SHELL, PAD, COLS), BF16),
            pltpu.VMEM((2 * PAD, COLS), BF16),
            pltpu.VMEM((6, DEEP, COLS), BF16),
            pltpu.VMEM((2 * PAD, PAD), F32),
            pltpu.VMEM((2 * PAD, DEEP), F32),
            pltpu.VMEM((3, PAD, DEEP), BF16),
            pltpu.VMEM((3, PAD, DEEP), BF16),
            pltpu.SemaphoreType.DMA((SHELL,)),
            pltpu.SemaphoreType.DMA,
            pltpu.SemaphoreType.DMA,
            pltpu.SemaphoreType.DMA((6, 2)),
            pltpu.SemaphoreType.DMA((2 * SHELL,)),
            pltpu.SemaphoreType.DMA((4, 3, 2)),
            pltpu.SemaphoreType.DMA((6,)),
            pltpu.SemaphoreType.DMA((6,)),
            pltpu.SemaphoreType.DMA,
            pltpu.SemaphoreType.DMA,
        ],
        compiler_params=pltpu.CompilerParams(
            collective_id=0, has_side_effects=True, vmem_limit_bytes=60 * 1024 * 1024
        ),
        name="disentangle",
    )(window_count, shell_weights, margins[0], subspace)


def solution(mesh):
    return jax.shard_map(
        on_device,
        mesh=mesh,
        in_specs=(P("kpt", None, "band", None), P("kpt", "band", None), P(), P("kpt")),
        out_specs=P("kpt", "band", None),
        check_vma=False,
    )
```

time: 349 us -> 84.4 us (0.24)
  waiting for transfers between devices: 223 us -> 0 us
  Pallas kernels: 0 us -> 81.8 us
  matrix products: 47.3 us -> 0 us
  blocking collectives: 25.8 us -> 0 us
  starting transfers between devices: 22.8 us -> 0 us
  between operations: 15.1 us -> 0.66 us
  other arithmetic: 8.28 us -> 0 us
  local copies, waits for them, and re-layouts: 5.6 us -> 1.78 us
    all_gather x2 -> x0, waiting for transfers between devices: 161 us -> none  [the longest x1 93.8 us: rows_first(): out = lax.all_gather(both, axis, axis=0, tiled=True)]
    pallas_call x0 -> x1, Pallas kernels: none -> 81.8 us  [on_device(): pl.pallas_call(kernel, out_shape=jax.ShapeDtypeStruct((1, ROWS, COLS), F3...]
    ppermute x10 -> x0, waiting for transfers between devices: 61.4 us -> none  [from_behind(): return lax.ppermute(value, axis, pairs)]
    dot_general x8 -> x0, matrix products: 47.3 us -> none  [the longest x1 25.7 us: assemble(): jnp.einsum('b,brs->rs', weights, products, precision=lax.Precision.HIGHEST)]
    all_to_all x2 -> x0, blocking collectives: 25.8 us -> none  [copy_for_each(): return lax.all_to_all(copies, axis, split_axis=0, concat_axis=0, tiled=True)]
    ppermute x10 -> x0, starting transfers between devices: 22.5 us -> none  [from_behind(): return lax.ppermute(value, axis, pairs)]
  transfers between devices with their start and end apart: 12 -> 0, of which waited for: 11 -> 0; matrix products, arithmetic and copies ran while one was open for 1% -> 0% of each run, Pallas kernels for 0% -> 0%
where the time goes in v1:
time: 84.4 us; the launch traced here: 84.3 us
  Pallas kernels  81.8 us (97%)
  local copies, waits for them, and re-layouts  1.78 us (2%)
    pallas_call x1, Pallas kernels, on_device(): pl.pallas_call(kernel, out_shape=jax.ShapeDtypeStruct((1, ROWS, COLS), F3...  81.8 us
    unnamed x1, local copies, waits for them, and re-layouts  1.78 us

profile of v1, /device:TPU:8, one launch (start us, length us, event | category | flops | bytes accessed | tf_op | source)
XLA Modules:
  0.0 84.3 jit_solution(16393668379331665894)
XLA Ops:
  0.7 81.8 %disentangle.1 = f32[1,200,512]{2,1,0:T(8,128)} custom-call(s32[1]{0:T(128)S(6)} %copy.6.window_ref, f32[12]{0:T(128)} %weight_ref.1, bf16[12,200,800]{2,1,0:T(8,128)(2,1)} %bitcast.1, bf16[1,200,512]{2,1,0:T(8,128)(2,1)} %own_ref.1), custom_call_target="tpu_custom_call" | custom-call | tf_op jit(solution)/shard_map/disentangle/pallas_call | solution.py:312
  82.5 1.8 %copy.7 = f32[1,200,512]{2,1,0:T(8,128)} copy(f32[1,200,512]{2,1,0:T(8,128)} %disentangle.1) | data formatting | bytes 819200

commit v2 on v1

v2 whole, which is shorter than its diff:
```python
import functools
import math

import jax
import jax.numpy as jnp
from jax import lax
from jax.experimental import pallas as pl
from jax.experimental.pallas import tpu as pltpu
from jax.sharding import PartitionSpec as P

SIZE_X, SIZE_Y, SIZE_Z = 4, 4, 8
ROWS = 200
PAD = 208
DEEP = 256
COLS = 512
HALF = 256
SHELL = 12
GIFTS = 3
MESH = pl.DeviceIdType.MESH
F32 = jnp.float32
BF16 = jnp.bfloat16

SHARED = 6
SLOTS = 9


def dot(a, b):
    return jnp.dot(a, b, preferred_element_type=F32)


def dot_nt(a, b):
    return lax.dot_general(a, b, (((1,), (1,)), ((), ())), preferred_element_type=F32)


def dot_tn(a, b):
    return lax.dot_general(a, b, (((0,), (0,)), ((), ())), preferred_element_type=F32)


def halves(a):
    high = a.astype(BF16)
    return high, (a - high.astype(F32)).astype(BF16)


def dot3(a, b, product=dot):
    a_high, a_low = halves(a)
    b_high, b_low = halves(b)
    return product(a_high, b_high) + (product(a_high, b_low) + product(a_low, b_high))


def complex_rows(both, rows, start):
    upper, lower = both[:rows], both[start:start + rows]
    return jnp.concatenate(
        [upper[:, :HALF] - lower[:, HALF:], upper[:, HALF:] + lower[:, :HALF]], axis=1
    )


def stack_complex(real, imag):
    return jnp.concatenate(
        [jnp.concatenate([real, imag], axis=1), jnp.concatenate([-imag, real], axis=1)], axis=0
    )


def unpacked_dots(block, upper, strict, subspace):
    block = block.astype(F32)
    real = jnp.where(upper, block, 0.0).astype(BF16)
    above = jnp.where(strict, block, 0.0).astype(BF16)
    imag = jnp.where(upper, 0.0, block).astype(BF16)
    plain = dot(jnp.concatenate([real, imag], axis=0), subspace)
    turned = dot_tn(jnp.concatenate([above, -imag], axis=1), subspace[:PAD])
    return plain, turned


def kernel(
    window_ref, weight_ref, margin_ref, own_ref, out_ref,
    raw, split, near, mine, alien, rotated, theirs, diag, other_diag, cross, packed, arrived,
    raw_sem, first_send, first_recv, gift_send, gift_recv, block_send, block_recv, relay_send,
    proj_send, proj_recv, z_send, z_recv,
):
    kpt = lax.axis_index("kpt")
    band = lax.axis_index("band")
    other = 1 - band
    i = lax.div(kpt, SIZE_Y * SIZE_Z)
    j = lax.rem(lax.div(kpt, SIZE_Z), SIZE_Y)
    l = lax.rem(kpt, SIZE_Z)
    odd = lax.rem(l, 2)
    minus = lax.rem(band + odd + lax.div(l, 2), 2)
    sign = 1 - 2 * minus

    def point(di, dj, new_l):
        new_i = lax.rem(i + di + SIZE_X, SIZE_X)
        new_j = lax.rem(j + dj + SIZE_Y, SIZE_Y)
        return (new_i * SIZE_Y + new_j) * SIZE_Z + new_l

    l_near = l + 1 - 2 * odd
    l_far = lax.rem(l + 2 * odd - 1 + SIZE_Z, SIZE_Z)
    l_hop = lax.rem(l + 2 - 4 * odd + SIZE_Z, SIZE_Z)
    l_back = lax.rem(l - 2 + 4 * odd + SIZE_Z, SIZE_Z)

    takers = [
        (point(sign, 0, l_near), band), (point(-sign, 0, l_near), band),
        (point(0, sign, l_near), band), (point(0, -sign, l_near), band),
        (point(sign, 0, l_far), other), (point(-sign, 0, l_far), other),
    ]
    hop_peer = (point(0, 0, l_hop), other)
    back_peer = (point(0, 0, l_back), other)
    partner = (kpt, other)

    plus = 1 - minus
    shell = [
        4 + 2 * minus + odd, 4 + 2 * plus + odd, 8 + 2 * minus + odd, 8 + 2 * plus + odd,
        5 + 2 * minus - odd, 5 + 2 * plus - odd, 1 + minus, 3 * plus, 9 + 2 * minus - odd,
    ]
    gift_shell = [1 + plus, 3 * minus, 9 + 2 * plus - odd]
    weights = [weight_ref[b] for b in shell]

    def weight_of(s):
        found = weights[0]
        for n in range(1, SLOTS):
            found = jnp.where(s == n, weights[n], found)
        return found

    loads = [
        pltpu.make_async_copy(margin_ref.at[shell[s]], raw.at[s], raw_sem.at[s]) for s in range(SLOTS)
    ]
    for load in loads:
        load.start()

    def clear(s, carry):
        near[s, ROWS:] = jnp.zeros((DEEP - ROWS, COLS), BF16)
        return carry

    lax.fori_loop(0, 2 * SLOTS + 2, clear, 0)
    theirs[:, PAD:] = jnp.zeros((3, DEEP - PAD, COLS), BF16)

    barrier = pltpu.get_barrier_semaphore()
    peers = takers + [hop_peer, back_peer, partner]
    for peer in peers:
        pl.semaphore_signal(barrier, inc=1, device_id=peer, device_id_type=MESH)
    pl.semaphore_wait(barrier, len(peers))

    def remote(src, dst, send_sem, recv_sem, peer):
        return pltpu.make_async_remote_copy(
            src_ref=src, dst_ref=dst, send_sem=send_sem, recv_sem=recv_sem, device_id=peer, device_id_type=MESH
        )

    def block(s, q):
        return near.at[2 * s + q, pl.ds(0, ROWS)]

    def wait_block(s, q):
        remote(block(s, q), block(s, q), block_send.at[0, 0], block_recv.at[2 * s + q], partner).wait_recv()

    u_own = own_ref.at[0]
    u_other = near.at[2 * SLOTS + 1, pl.ds(0, ROWS)]
    sent = []

    def direct(s, src, q, turn):
        copy = remote(src, block(s, q), block_send.at[s, turn], block_recv.at[2 * s + q], takers[s])
        copy.start()
        sent.append(copy)

    first = remote(u_own, u_other, first_send, first_recv, partner)
    first.start()
    for s in (2, 0, 1, 3, 4, 5):
        direct(s, u_own, band, 0)
    gifts = [
        remote(margin_ref.at[gift_shell[n]], raw.at[SLOTS + n], gift_send.at[n], gift_recv.at[n], partner)
        for n in range(GIFTS)
    ]
    for gift in gifts:
        gift.start()

    near[2 * SLOTS, :ROWS] = own_ref[0]
    diag[...] = jnp.zeros_like(diag)
    other_diag[...] = jnp.zeros_like(other_diag)
    cross[...] = jnp.zeros_like(cross)
    split[...] = jnp.zeros_like(split)
    for load in loads:
        load.wait()

    def separate(s, carry):
        whole = raw[s]
        for part in range(4):
            piece = whole[:, part * ROWS:(part + 1) * ROWS]
            split[2 * s + part % 2, (part // 2) * PAD:(part // 2) * PAD + ROWS, :ROWS] = piece
        return carry

    lax.fori_loop(0, 4, separate, 0)

    first.wait_recv()
    for s in (2, 0, 1, 3, 4, 5):
        direct(s, u_other, other, 1)

    def relays(q, turn):
        targets = ((6, takers[0]), (7, takers[1]), (8, hop_peer))
        return [
            remote(block(2, q), block(target, q), relay_send.at[n, turn], block_recv.at[2 * target + q], peer)
            for n, (target, peer) in enumerate(targets)
        ]

    wait_block(2, band)
    for copy in relays(band, 0):
        copy.start()
    lax.fori_loop(4, SLOTS, separate, 0)
    wait_block(2, other)
    for copy in relays(other, 1):
        copy.start()

    row = lax.broadcasted_iota(jnp.int32, (PAD, 1), 0)

    def projection(margin, s, owner):
        both = dot(split[2 * margin], near[2 * s]) + dot(split[2 * margin + 1], near[2 * s + 1])
        inside = (row < ROWS) & (row + owner * ROWS < window_ref[0])
        return jnp.where(inside, complex_rows(both, PAD, PAD), 0.0).astype(BF16)

    def turn_by(projected):
        rotated[0:PAD] = projected
        rotated[PAD:, :HALF] = projected[:, HALF:]
        rotated[PAD:, HALF:] = -projected[:, :HALF]

    def project(s, carry):
        projected = projection(s, s, band)
        mine[s] = projected
        turn_by(projected)
        diag[...] += weight_of(s) * dot_nt(rotated[...], projected)
        return carry

    def project_all(s, carry):
        aliens = projection(s + GIFTS, s, other)
        weight = weight_of(s)
        turn_by(aliens)
        other_diag[...] += weight * dot_nt(rotated[...], aliens)
        alien[0:PAD] = aliens
        projected = projection(s, s, band)
        turn_by(projected)
        diag[...] += weight * dot_nt(rotated[...], projected)
        cross[...] += weight * dot_nt(rotated[...], alien[...])
        return carry

    def proj_copy(t):
        return remote(
            mine.at[2 * t], theirs.at[t, pl.ds(0, PAD)], proj_send.at[t], proj_recv.at[t], partner
        )

    def meet(t):
        proj_copy(t).wait_recv()
        turn_by(mine[2 * t + 1])
        cross[...] += weight_of(2 * t + 1) * dot_nt(rotated[...], theirs[t])

    alien[PAD:] = jnp.zeros((DEEP - PAD, COLS), BF16)

    def pair(t, carry):
        for u in range(2):
            @pl.when((t != 1) | (u == 1))
            def _():
                for q in range(2):
                    wait_block(2 * t + u, q)

        lax.fori_loop(2 * t, 2 * t + 2, project, 0)
        proj_copy(t).start()
        return carry

    lax.fori_loop(0, SHARED // 2, pair, 0)

    def swapped(n, carry):
        remote(margin_ref.at[n], raw.at[SLOTS + n], gift_send.at[n], gift_recv.at[n], partner).wait_recv()
        separate(SLOTS + n, 0)
        for q in range(2):
            wait_block(SHARED + n, q)
        project_all(SHARED + n, 0)
        return carry

    lax.fori_loop(0, GIFTS, swapped, 0)

    place_row = lax.broadcasted_iota(jnp.int32, (PAD, DEEP), 0)
    place_col = lax.broadcasted_iota(jnp.int32, (PAD, DEEP), 1)
    upper = place_row <= place_col
    strict = place_row < place_col
    for n, ref in enumerate((diag, other_diag)):
        packed[n, :, :PAD] = jnp.where(upper[:, :PAD], ref[:PAD], ref[PAD:]).astype(BF16)
        packed[n, :, PAD:] = jnp.zeros((PAD, DEEP - PAD), BF16)
    swap = [
        remote(packed.at[pl.ds(2 * n, 2)], arrived.at[pl.ds(2 * n, 2)], z_send.at[n], z_recv.at[n], partner)
        for n in range(2)
    ]
    swap[0].start()

    def meet_all(t, carry):
        meet(t)
        return carry

    lax.fori_loop(0, SHARED // 2, meet_all, 0)
    packed[2] = cross[:PAD].astype(BF16)
    packed[3] = cross[PAD:].astype(BF16)
    swap[1].start()

    u_h = near[2 * SLOTS]
    u_o = near[2 * SLOTS + 1]
    diag_high, diag_low = halves(diag[...])
    alien_high, alien_low = halves(other_diag[...])
    cross_high, cross_low = halves(cross[...])
    x_h = dot(diag_high, u_h[:PAD]) + dot(diag_low, u_h[:PAD]) + (dot(cross_high, u_o) + dot(cross_low, u_o))
    x_o = dot(alien_high, u_o[:PAD]) + dot(alien_low, u_o[:PAD])
    flipped_high = jnp.concatenate([cross_high[:PAD], -cross_high[PAD:]], axis=1)
    flipped_low = jnp.concatenate([cross_low[:PAD], -cross_low[PAD:]], axis=1)
    x_o_turned = dot_tn(flipped_high, u_h[:PAD]) + dot_tn(flipped_low, u_h[:PAD])

    swap[0].wait_recv()
    plain, turned = unpacked_dots(arrived[0], upper, strict, u_o)
    x_o = x_o + plain
    x_o_turned = x_o_turned + turned
    plain, x_h_turned = unpacked_dots(arrived[1], upper, strict, u_h)
    x_h = x_h + plain

    swap[1].wait_recv()
    real, imag = arrived[2], arrived[3]
    x_h_turned = x_h_turned + dot_tn(jnp.concatenate([real, -imag], axis=1), u_o[:PAD])
    x_o = x_o + dot(jnp.concatenate([real, imag], axis=0), u_h)
    x_h = complex_rows(x_h, PAD, PAD) + complex_rows(x_h_turned, PAD, DEEP)
    x_o = complex_rows(x_o, PAD, PAD) + complex_rows(x_o_turned, PAD, DEEP)

    x_all = jnp.concatenate([x_h, x_o], axis=0)
    squares = jnp.sum(jnp.sum(x_all * x_all, axis=0, keepdims=True), axis=1, keepdims=True)
    scale = lax.rsqrt(2.0 * squares / HALF + 1e-06)
    gram = dot3(x_all, x_all, dot_tn) * (scale * scale)
    gram_real = gram[:HALF, :HALF] + gram[HALF:, HALF:]
    gram_imag = gram[:HALF, HALF:] - gram[HALF:, :HALF]
    eye = (
        lax.broadcasted_iota(jnp.int32, (HALF, HALF), 0) == lax.broadcasted_iota(jnp.int32, (HALF, HALF), 1)
    ).astype(F32)
    factor = stack_complex(1.5 * eye - 0.5 * gram_real, -0.5 * gram_imag)
    stacked = jnp.concatenate([x_h, jnp.concatenate([gram_real, gram_imag], axis=1)], axis=0)
    stacked = dot3(stacked, factor)
    gram = dot3(stacked[PAD:], factor)
    factor = stack_complex(1.5 * eye - 0.5 * gram[:, :HALF], -0.5 * gram[:, HALF:])
    out_ref[0] = (dot3(stacked[:PAD], factor) * (scale * math.sqrt(2.0 * ROWS)))[:ROWS]

    first.wait_send()
    for copy in sent + gifts + relays(band, 0) + relays(other, 1) + swap:
        copy.wait_send()
    for t in range(SHARED // 2):
        proj_copy(t).wait_send()


def on_device(margins, subspace, shell_weights, window_count):
    vmem = pl.BlockSpec(memory_space=pltpu.VMEM)
    smem = pl.BlockSpec(memory_space=pltpu.SMEM)
    return pl.pallas_call(
        kernel,
        out_shape=jax.ShapeDtypeStruct((1, ROWS, COLS), F32),
        in_specs=[smem, smem, pl.BlockSpec(memory_space=pl.ANY), vmem],
        out_specs=vmem,
        scratch_shapes=[
            pltpu.VMEM((SHELL, ROWS, 4 * ROWS), BF16),
            pltpu.VMEM((2 * SHELL, 2 * PAD, DEEP), BF16),
            pltpu.VMEM((2 * SLOTS + 2, DEEP, COLS), BF16),
            pltpu.VMEM((SHARED, PAD, COLS), BF16),
            pltpu.VMEM((DEEP, COLS), BF16),
            pltpu.VMEM((2 * PAD, COLS), BF16),
            pltpu.VMEM((SHARED // 2, DEEP, COLS), BF16),
            pltpu.VMEM((2 * PAD, PAD), F32),
            pltpu.VMEM((2 * PAD, PAD), F32),
            pltpu.VMEM((2 * PAD, DEEP), F32),
            pltpu.VMEM((4, PAD, DEEP), BF16),
            pltpu.VMEM((4, PAD, DEEP), BF16),
            pltpu.SemaphoreType.DMA((SLOTS,)),
            pltpu.SemaphoreType.DMA,
            pltpu.SemaphoreType.DMA,
            pltpu.SemaphoreType.DMA((GIFTS,)),
            pltpu.SemaphoreType.DMA((GIFTS,)),
            pltpu.SemaphoreType.DMA((6, 2)),
            pltpu.SemaphoreType.DMA((2 * SLOTS,)),
            pltpu.SemaphoreType.DMA((3, 2)),
            pltpu.SemaphoreType.DMA((SHARED // 2,)),
            pltpu.SemaphoreType.DMA((SHARED // 2,)),
            pltpu.SemaphoreType.DMA((2,)),
            pltpu.SemaphoreType.DMA((2,)),
        ],
        compiler_params=pltpu.CompilerParams(
            collective_id=0, has_side_effects=True, vmem_limit_bytes=60 * 1024 * 1024
        ),
        name="disentangle",
    )(window_count, shell_weights, margins[0], subspace)


def solution(mesh):
    return jax.shard_map(
        on_device,
        mesh=mesh,
        in_specs=(P("kpt", None, "band", None), P("kpt", "band", None), P(), P("kpt")),
        out_specs=P("kpt", "band", None),
        check_vma=False,
    )
```

time: 84.4 us -> 68 us (0.81)
  Pallas kernels: 81.8 us -> 64.7 us
    pallas_call x1, Pallas kernels: 81.8 us -> 64.7 us  [on_device(): pl.pallas_call(kernel, out_shape=jax.ShapeDtypeStruct((1, ROWS, COLS), F3...]
where the time goes in v2:
time: 68 us; the launch traced here: 67.2 us
  Pallas kernels  64.7 us (95%)
  local copies, waits for them, and re-layouts  1.78 us (3%)
    pallas_call x1, Pallas kernels, on_device(): pl.pallas_call(kernel, out_shape=jax.ShapeDtypeStruct((1, ROWS, COLS), F3...  64.7 us
    unnamed x1, local copies, waits for them, and re-layouts  1.78 us

profile of v2, /device:TPU:8, one launch (start us, length us, event | category | flops | bytes accessed | tf_op | source)
XLA Modules:
  0.0 67.2 jit_solution(12253026287419239162)
XLA Ops:
  0.7 64.7 %disentangle.1 = f32[1,200,512]{2,1,0:T(8,128)} custom-call(s32[1]{0:T(128)S(6)} %copy.6.window_ref, f32[12]{0:T(128)} %weight_ref.1, bf16[12,200,800]{2,1,0:T(8,128)(2,1)} %bitcast.1, bf16[1,200,512]{2,1,0:T(8,128)(2,1)} %own_ref.1), custom_call_target="tpu_custom_call" | custom-call | tf_op jit(solution)/shard_map/disentangle/pallas_call | solution.py:347
  65.4 1.8 %copy.7 = f32[1,200,512]{2,1,0:T(8,128)} copy(f32[1,200,512]{2,1,0:T(8,128)} %disentangle.1) | data formatting | bytes 819200

commit v3 on v2

--- a/solution.py
+++ b/solution.py
@@ -15,13 +15,18 @@
 COLS = 512
 HALF = 256
 SHELL = 12
-GIFTS = 3
+GIFTS = 4
+STEM = 768
+TAIL = 4 * ROWS - STEM
+WIDE = 384
+REST = 2 * ROWS - WIDE
 MESH = pl.DeviceIdType.MESH
 F32 = jnp.float32
 BF16 = jnp.bfloat16
 
-SHARED = 6
-SLOTS = 9
+SHARED = 4
+SLOTS = 8
+FAR = SLOTS + 1
 
 
 def dot(a, b):
@@ -72,8 +77,8 @@
 
 def kernel(
     window_ref, weight_ref, margin_ref, own_ref, out_ref,
-    raw, split, near, mine, alien, rotated, theirs, diag, other_diag, cross, packed, arrived,
-    raw_sem, first_send, first_recv, gift_send, gift_recv, block_send, block_recv, relay_send,
+    raw, spare, tails, given, split, near, mine, alien, rotated, theirs, diag, other_diag, cross, packed, arrived,
+    own_sem, raw_sem, first_send, first_recv, gift_send, gift_recv, block_send, block_recv,
     proj_send, proj_recv, z_send, z_recv,
 ):
     kpt = lax.axis_index("kpt")
@@ -98,19 +103,20 @@
 
     takers = [
         (point(sign, 0, l_near), band), (point(-sign, 0, l_near), band),
-        (point(0, sign, l_near), band), (point(0, -sign, l_near), band),
-        (point(sign, 0, l_far), other), (point(-sign, 0, l_far), other),
+        (point(0, sign, l_near), band),
     ]
+    far_peer = (point(0, 0, l_far), other)
+    far_takers = [(point(-sign, 0, l), band), (point(sign, 0, l), band)]
     hop_peer = (point(0, 0, l_hop), other)
     back_peer = (point(0, 0, l_back), other)
     partner = (kpt, other)
 
     plus = 1 - minus
     shell = [
-        4 + 2 * minus + odd, 4 + 2 * plus + odd, 8 + 2 * minus + odd, 8 + 2 * plus + odd,
-        5 + 2 * minus - odd, 5 + 2 * plus - odd, 1 + minus, 3 * plus, 9 + 2 * minus - odd,
+        4 + 2 * minus + odd, 4 + 2 * plus + odd, 5 + 2 * minus - odd, 5 + 2 * plus - odd,
+        8 + 2 * minus + odd, 1 + minus, 3 * plus, 9 + 2 * minus - odd,
     ]
-    gift_shell = [1 + plus, 3 * minus, 9 + 2 * plus - odd]
+    gift_shell = [8 + 2 * plus + odd, 1 + plus, 3 * minus, 9 + 2 * plus - odd]
     weights = [weight_ref[b] for b in shell]
 
     def weight_of(s):
@@ -122,7 +128,13 @@
     loads = [
         pltpu.make_async_copy(margin_ref.at[shell[s]], raw.at[s], raw_sem.at[s]) for s in range(SLOTS)
     ]
-    for load in loads:
+    u_own = near.at[2 * SLOTS, pl.ds(0, ROWS)]
+    own_load = pltpu.make_async_copy(own_ref.at[0], u_own, own_sem)
+    own_load.start()
+    gift_loads = [
+        pltpu.make_async_copy(margin_ref.at[gift_shell[n]], spare.at[n], raw_sem.at[SLOTS + n]) for n in range(GIFTS)
+    ]
+    for load in loads + gift_loads:
         load.start()
 
     def clear(s, carry):
@@ -130,10 +142,10 @@
         return carry
 
     lax.fori_loop(0, 2 * SLOTS + 2, clear, 0)
-    theirs[:, PAD:] = jnp.zeros((3, DEEP - PAD, COLS), BF16)
+    theirs[:, ROWS:] = jnp.zeros((SHARED // 2, DEEP - ROWS, COLS), BF16)
 
     barrier = pltpu.get_barrier_semaphore()
-    peers = takers + [hop_peer, back_peer, partner]
+    peers = takers + far_takers + [far_peer, hop_peer, back_peer, partner]
     for peer in peers:
         pl.semaphore_signal(barrier, inc=1, device_id=peer, device_id_type=MESH)
     pl.semaphore_wait(barrier, len(peers))
@@ -147,35 +159,45 @@
         return near.at[2 * s + q, pl.ds(0, ROWS)]
 
     def wait_block(s, q):
-        remote(block(s, q), block(s, q), block_send.at[0, 0], block_recv.at[2 * s + q], partner).wait_recv()
-
-    u_own = own_ref.at[0]
+        remote(block(s, q), block(s, q), block_send.at[0], block_recv.at[2 * s + q], partner).wait_recv()
+
     u_other = near.at[2 * SLOTS + 1, pl.ds(0, ROWS)]
     sent = []
 
-    def direct(s, src, q, turn):
-        copy = remote(src, block(s, q), block_send.at[s, turn], block_recv.at[2 * s + q], takers[s])
+    def pass_on(src, s, q, turn, peer):
+        copy = remote(src, block(s, q), block_send.at[2 * s + turn], block_recv.at[2 * s + q], peer)
         copy.start()
         sent.append(copy)
 
     first = remote(u_own, u_other, first_send, first_recv, partner)
+    own_load.wait()
     first.start()
-    for s in (2, 0, 1, 3, 4, 5):
-        direct(s, u_own, band, 0)
+    def offer(src, q, turn):
+        pass_on(src, 4, q, turn, takers[2])
+        pass_on(src, FAR, q, turn, far_peer)
+        for s in (0, 1):
+            pass_on(src, s, q, turn, takers[s])
+
+    offer(u_own, band, 0)
     gifts = [
-        remote(margin_ref.at[gift_shell[n]], raw.at[SLOTS + n], gift_send.at[n], gift_recv.at[n], partner)
+        remote(
+            margin_ref.at[gift_shell[n], :, pl.ds(0, STEM)], raw.at[SLOTS + n, :, pl.ds(0, STEM)], gift_send.at[n],
+            gift_recv.at[n], partner,
+        )
         for n in range(GIFTS)
     ]
+    tail_gift = remote(tails, given, gift_send.at[GIFTS], gift_recv.at[GIFTS], partner)
     for gift in gifts:
         gift.start()
 
-    near[2 * SLOTS, :ROWS] = own_ref[0]
     diag[...] = jnp.zeros_like(diag)
     other_diag[...] = jnp.zeros_like(other_diag)
     cross[...] = jnp.zeros_like(cross)
     split[...] = jnp.zeros_like(split)
-    for load in loads:
+    for load in loads + gift_loads:
         load.wait()
+    for n in range(GIFTS):
+        tails[:, n * TAIL:(n + 1) * TAIL] = spare[n, :, STEM:]
 
     def separate(s, carry):
         whole = raw[s]
@@ -185,25 +207,21 @@
         return carry
 
     lax.fori_loop(0, 4, separate, 0)
+    tail_gift.start()
 
     first.wait_recv()
-    for s in (2, 0, 1, 3, 4, 5):
-        direct(s, u_other, other, 1)
-
-    def relays(q, turn):
-        targets = ((6, takers[0]), (7, takers[1]), (8, hop_peer))
-        return [
-            remote(block(2, q), block(target, q), relay_send.at[n, turn], block_recv.at[2 * target + q], peer)
-            for n, (target, peer) in enumerate(targets)
-        ]
-
-    wait_block(2, band)
-    for copy in relays(band, 0):
-        copy.start()
-    lax.fori_loop(4, SLOTS, separate, 0)
-    wait_block(2, other)
-    for copy in relays(other, 1):
-        copy.start()
+    offer(u_other, other, 1)
+
+    for turn, q in enumerate((band, other)):
+        wait_block(FAR, q)
+        for n in range(2):
+            pass_on(block(FAR, q), 2 + n, q, turn, far_takers[n])
+        wait_block(4, q)
+        for n in range(2):
+            pass_on(block(4, q), 5 + n, q, turn, takers[n])
+        pass_on(block(4, q), 7, q, turn, hop_peer)
+        if turn == 0:
+            lax.fori_loop(4, SLOTS, separate, 0)
 
     row = lax.broadcasted_iota(jnp.int32, (PAD, 1), 0)
 
@@ -238,7 +256,7 @@
 
     def proj_copy(t):
         return remote(
-            mine.at[2 * t], theirs.at[t, pl.ds(0, PAD)], proj_send.at[t], proj_recv.at[t], partner
+            mine.at[2 * t, pl.ds(0, ROWS)], theirs.at[t, pl.ds(0, ROWS)], proj_send.at[t], proj_recv.at[t], partner
         )
 
     def meet(t):
@@ -249,39 +267,62 @@
     alien[PAD:] = jnp.zeros((DEEP - PAD, COLS), BF16)
 
     def pair(t, carry):
-        for u in range(2):
-            @pl.when((t != 1) | (u == 1))
-            def _():
-                for q in range(2):
-                    wait_block(2 * t + u, q)
-
         lax.fori_loop(2 * t, 2 * t + 2, project, 0)
         proj_copy(t).start()
         return carry
 
-    lax.fori_loop(0, SHARED // 2, pair, 0)
+    def wait_pair(t, carry):
+        for u in range(2):
+            for q in range(2):
+                wait_block(2 * t + u, q)
+        return carry
+
+    def shared(t, carry):
+        wait_pair(t, 0)
+        return pair(t, carry)
 
     def swapped(n, carry):
-        remote(margin_ref.at[n], raw.at[SLOTS + n], gift_send.at[n], gift_recv.at[n], partner).wait_recv()
         separate(SLOTS + n, 0)
-        for q in range(2):
-            wait_block(SHARED + n, q)
+
+        @pl.when(n > 0)
+        def _():
+            for q in range(2):
+                wait_block(SHARED + n, q)
+
         project_all(SHARED + n, 0)
         return carry
 
+    lax.fori_loop(0, SHARED // 2, shared, 0)
+    tail_gift.wait_recv()
+    for n in range(GIFTS):
+        gifts[n].wait_recv()
+        raw[SLOTS + n, :, STEM:] = given[:, n * TAIL:(n + 1) * TAIL]
     lax.fori_loop(0, GIFTS, swapped, 0)
 
     place_row = lax.broadcasted_iota(jnp.int32, (PAD, DEEP), 0)
     place_col = lax.broadcasted_iota(jnp.int32, (PAD, DEEP), 1)
     upper = place_row <= place_col
     strict = place_row < place_col
-    for n, ref in enumerate((diag, other_diag)):
-        packed[n, :, :PAD] = jnp.where(upper[:, :PAD], ref[:PAD], ref[PAD:]).astype(BF16)
-        packed[n, :, PAD:] = jnp.zeros((PAD, DEEP - PAD), BF16)
-    swap = [
-        remote(packed.at[pl.ds(2 * n, 2)], arrived.at[pl.ds(2 * n, 2)], z_send.at[n], z_recv.at[n], partner)
-        for n in range(2)
-    ]
+    pick = (
+        lax.broadcasted_iota(jnp.int32, (REST, DEEP), 1) == ROWS - REST + lax.broadcasted_iota(jnp.int32, (REST, DEEP), 0)
+    ).astype(BF16)
+
+    def pack(n, left, right):
+        left, right = left.astype(BF16), right.astype(BF16)
+        packed[n, :PAD] = jnp.concatenate([left[:, :ROWS], right[:, :ROWS - REST]], axis=1)
+        packed[n, PAD:, :PAD] = dot_nt(pick[:, :PAD], right).astype(BF16)
+
+    def unpack(n):
+        both = arrived[n, :PAD]
+        left = jnp.where(place_col < ROWS, both[:, :DEEP].astype(F32), 0.0).astype(BF16)
+        shifted = jnp.concatenate([both[:, ROWS:], jnp.zeros((PAD, DEEP - WIDE + ROWS), BF16)], axis=1)
+        rest = dot_tn(arrived[n, PAD:, :PAD], pick)
+        return left, (shifted.astype(F32) + rest).astype(BF16)
+
+    packed[:, PAD:] = jnp.zeros((2, REST, WIDE), BF16)
+    square = upper[:, :PAD]
+    pack(0, jnp.where(square, diag[:PAD], diag[PAD:]), jnp.where(square, other_diag[:PAD], other_diag[PAD:]))
+    swap = [remote(packed.at[n], arrived.at[n], z_send.at[n], z_recv.at[n], partner) for n in range(2)]
     swap[0].start()
 
     def meet_all(t, carry):
@@ -289,8 +330,7 @@
         return carry
 
     lax.fori_loop(0, SHARED // 2, meet_all, 0)
-    packed[2] = cross[:PAD].astype(BF16)
-    packed[3] = cross[PAD:].astype(BF16)
+    pack(1, cross[:PAD, :PAD], cross[PAD:, :PAD])
     swap[1].start()
 
     u_h = near[2 * SLOTS]
@@ -305,14 +345,15 @@
     x_o_turned = dot_tn(flipped_high, u_h[:PAD]) + dot_tn(flipped_low, u_h[:PAD])
 
     swap[0].wait_recv()
-    plain, turned = unpacked_dots(arrived[0], upper, strict, u_o)
+    theirs_own, theirs_other = unpack(0)
+    plain, turned = unpacked_dots(theirs_own, upper, strict, u_o)
     x_o = x_o + plain
     x_o_turned = x_o_turned + turned
-    plain, x_h_turned = unpacked_dots(arrived[1], upper, strict, u_h)
+    plain, x_h_turned = unpacked_dots(theirs_other, upper, strict, u_h)
     x_h = x_h + plain
 
     swap[1].wait_recv()
-    real, imag = arrived[2], arrived[3]
+    real, imag = unpack(1)
     x_h_turned = x_h_turned + dot_tn(jnp.concatenate([real, -imag], axis=1), u_o[:PAD])
     x_o = x_o + dot(jnp.concatenate([real, imag], axis=0), u_h)
     x_h = complex_rows(x_h, PAD, PAD) + complex_rows(x_h_turned, PAD, DEEP)
@@ -335,7 +376,7 @@
     out_ref[0] = (dot3(stacked[:PAD], factor) * (scale * math.sqrt(2.0 * ROWS)))[:ROWS]
 
     first.wait_send()
-    for copy in sent + gifts + relays(band, 0) + relays(other, 1) + swap:
+    for copy in sent + gifts + [tail_gift] + swap:
         copy.wait_send()
     for t in range(SHARED // 2):
         proj_copy(t).wait_send()
@@ -347,12 +388,15 @@
     return pl.pallas_call(
         kernel,
         out_shape=jax.ShapeDtypeStruct((1, ROWS, COLS), F32),
-        in_specs=[smem, smem, pl.BlockSpec(memory_space=pl.ANY), vmem],
+        in_specs=[smem, smem, pl.BlockSpec(memory_space=pl.ANY), pl.BlockSpec(memory_space=pl.ANY)],
         out_specs=vmem,
         scratch_shapes=[
             pltpu.VMEM((SHELL, ROWS, 4 * ROWS), BF16),
+            pltpu.VMEM((GIFTS, ROWS, 4 * ROWS), BF16),
+            pltpu.VMEM((ROWS, GIFTS * TAIL), BF16),
+            pltpu.VMEM((ROWS, GIFTS * TAIL), BF16),
             pltpu.VMEM((2 * SHELL, 2 * PAD, DEEP), BF16),
-            pltpu.VMEM((2 * SLOTS + 2, DEEP, COLS), BF16),
+            pltpu.VMEM((2 * SLOTS + 4, DEEP, COLS), BF16),
             pltpu.VMEM((SHARED, PAD, COLS), BF16),
             pltpu.VMEM((DEEP, COLS), BF16),
             pltpu.VMEM((2 * PAD, COLS), BF16),
@@ -360,16 +404,16 @@
             pltpu.VMEM((2 * PAD, PAD), F32),
             pltpu.VMEM((2 * PAD, PAD), F32),
             pltpu.VMEM((2 * PAD, DEEP), F32),
-            pltpu.VMEM((4, PAD, DEEP), BF16),
-            pltpu.VMEM((4, PAD, DEEP), BF16),
-            pltpu.SemaphoreType.DMA((SLOTS,)),
+            pltpu.VMEM((2, PAD + REST, WIDE), BF16),
+            pltpu.VMEM((2, PAD + REST, WIDE), BF16),
+            pltpu.SemaphoreType.DMA,
+            pltpu.SemaphoreType.DMA((SLOTS + GIFTS,)),
             pltpu.SemaphoreType.DMA,
             pltpu.SemaphoreType.DMA,
-            pltpu.SemaphoreType.DMA((GIFTS,)),
-            pltpu.SemaphoreType.DMA((GIFTS,)),
-            pltpu.SemaphoreType.DMA((6, 2)),
-            pltpu.SemaphoreType.DMA((2 * SLOTS,)),
-            pltpu.SemaphoreType.DMA((3, 2)),
+            pltpu.SemaphoreType.DMA((GIFTS + 1,)),
+            pltpu.SemaphoreType.DMA((GIFTS + 1,)),
+            pltpu.SemaphoreType.DMA((2 * FAR + 2,)),
+            pltpu.SemaphoreType.DMA((2 * FAR + 2,)),
             pltpu.SemaphoreType.DMA((SHARED // 2,)),
             pltpu.SemaphoreType.DMA((SHARED // 2,)),
             pltpu.SemaphoreType.DMA((2,)),

time: 68 us -> 65.8 us (0.968)
  the two profiles are of different devices: /device:TPU:8 before, /device:TPU:1 now
where the time goes in v3:
time: 65.8 us; the launch traced here: 65.6 us
  Pallas kernels  63.2 us (96%)
  local copies, waits for them, and re-layouts  1.78 us (3%)
  between operations  0.66 us (1%)
    pallas_call x1, Pallas kernels, on_device(): pl.pallas_call(kernel, out_shape=jax.ShapeDtypeStruct((1, ROWS, COLS), F3...  63.2 us
    unnamed x1, local copies, waits for them, and re-layouts  1.78 us

profile of v3, /device:TPU:1, one launch (start us, length us, event | category | flops | bytes accessed | tf_op | source)
XLA Modules:
  0.0 65.6 jit_solution(12969900617785194124)
XLA Ops:
  0.7 63.2 %disentangle.1 = f32[1,200,512]{2,1,0:T(8,128)} custom-call(s32[1]{0:T(128)S(6)} %copy.6.window_ref, f32[12]{0:T(128)} %weight_ref.1, bf16[12,200,800]{2,1,0:T(8,128)(2,1)} %bitcast.1, bf16[1,200,512]{2,1,0:T(8,128)(2,1)} %own_ref.1), custom_call_target="tpu_custom_call" | custom-call | tf_op jit(solution)/shard_map/disentangle/pallas_call | solution.py:388
  63.8 1.8 %copy.7 = f32[1,200,512]{2,1,0:T(8,128)} copy(f32[1,200,512]{2,1,0:T(8,128)} %disentangle.1) | data formatting | bytes 819200

commit v4 on v3

--- a/solution.py
+++ b/solution.py
@@ -187,8 +187,6 @@
         for n in range(GIFTS)
     ]
     tail_gift = remote(tails, given, gift_send.at[GIFTS], gift_recv.at[GIFTS], partner)
-    for gift in gifts:
-        gift.start()
 
     diag[...] = jnp.zeros_like(diag)
     other_diag[...] = jnp.zeros_like(other_diag)
@@ -206,8 +204,11 @@
             split[2 * s + part % 2, (part // 2) * PAD:(part // 2) * PAD + ROWS, :ROWS] = piece
         return carry
 
+    gifts[0].start()
     lax.fori_loop(0, 4, separate, 0)
     tail_gift.start()
+    for gift in gifts[1:]:
+        gift.start()
 
     first.wait_recv()
     offer(u_other, other, 1)
@@ -282,6 +283,8 @@
         return pair(t, carry)
 
     def swapped(n, carry):
+        stem = raw.at[SLOTS + n, :, pl.ds(0, STEM)]
+        remote(stem, stem, gift_send.at[n], gift_recv.at[n], partner).wait_recv()
         separate(SLOTS + n, 0)
 
         @pl.when(n > 0)
@@ -295,7 +298,6 @@
     lax.fori_loop(0, SHARED // 2, shared, 0)
     tail_gift.wait_recv()
     for n in range(GIFTS):
-        gifts[n].wait_recv()
         raw[SLOTS + n, :, STEM:] = given[:, n * TAIL:(n + 1) * TAIL]
     lax.fori_loop(0, GIFTS, swapped, 0)
 

time: 65.8 us -> 63.6 us (0.967)
  the two profiles are of different devices: /device:TPU:1 before, /device:TPU:8 now
where the time goes in v4:
time: 63.6 us; the launch traced here: 63.4 us
  Pallas kernels  61 us (96%)
  local copies, waits for them, and re-layouts  1.78 us (3%)
  between operations  0.66 us (1%)
    pallas_call x1, Pallas kernels, on_device(): pl.pallas_call(kernel, out_shape=jax.ShapeDtypeStruct((1, ROWS, COLS), F3...  61 us
    unnamed x1, local copies, waits for them, and re-layouts  1.78 us

profile of v4, /device:TPU:8, one launch (start us, length us, event | category | flops | bytes accessed | tf_op | source)
XLA Modules:
  0.0 63.4 jit_solution(5857497186765509830)
XLA Ops:
  0.7 61.0 %disentangle.1 = f32[1,200,512]{2,1,0:T(8,128)} custom-call(s32[1]{0:T(128)S(6)} %copy.6.window_ref, f32[12]{0:T(128)} %weight_ref.1, bf16[12,200,800]{2,1,0:T(8,128)(2,1)} %bitcast.1, bf16[1,200,512]{2,1,0:T(8,128)(2,1)} %own_ref.1), custom_call_target="tpu_custom_call" | custom-call | tf_op jit(solution)/shard_map/disentangle/pallas_call | solution.py:390
  61.7 1.8 %copy.7 = f32[1,200,512]{2,1,0:T(8,128)} copy(f32[1,200,512]{2,1,0:T(8,128)} %disentangle.1) | data formatting | bytes 819200

commit v5 on v4

--- a/solution.py
+++ b/solution.py
@@ -52,11 +52,12 @@
     return product(a_high, b_high) + (product(a_high, b_low) + product(a_low, b_high))
 
 
+def combine(real, imag):
+    return jnp.concatenate([real[:, :HALF] - imag[:, HALF:], real[:, HALF:] + imag[:, :HALF]], axis=1)
+
+
 def complex_rows(both, rows, start):
-    upper, lower = both[:rows], both[start:start + rows]
-    return jnp.concatenate(
-        [upper[:, :HALF] - lower[:, HALF:], upper[:, HALF:] + lower[:, :HALF]], axis=1
-    )
+    return combine(both[:rows], both[start:start + rows])
 
 
 def stack_complex(real, imag):
@@ -77,7 +78,7 @@
 
 def kernel(
     window_ref, weight_ref, margin_ref, own_ref, out_ref,
-    raw, spare, tails, given, split, near, mine, alien, rotated, theirs, diag, other_diag, cross, packed, arrived,
+    raw, spare, tails, given, split, near, mine, alien, rotated, theirs, diag, other_diag, cross, packed, arrived, lowered,
     own_sem, raw_sem, first_send, first_recv, gift_send, gift_recv, block_send, block_recv,
     proj_send, proj_recv, z_send, z_recv,
 ):
@@ -346,6 +347,9 @@
     flipped_low = jnp.concatenate([cross_low[:PAD], -cross_low[PAD:]], axis=1)
     x_o_turned = dot_tn(flipped_high, u_h[:PAD]) + dot_tn(flipped_low, u_h[:PAD])
 
+    lowered[:ROWS] = jnp.zeros((ROWS, COLS), BF16)
+    lowered[ROWS:] = u_h[:ROWS]
+
     swap[0].wait_recv()
     theirs_own, theirs_other = unpack(0)
     plain, turned = unpacked_dots(theirs_own, upper, strict, u_o)
@@ -354,12 +358,15 @@
     plain, x_h_turned = unpacked_dots(theirs_other, upper, strict, u_h)
     x_h = x_h + plain
 
-    swap[1].wait_recv()
-    real, imag = unpack(1)
-    x_h_turned = x_h_turned + dot_tn(jnp.concatenate([real, -imag], axis=1), u_o[:PAD])
-    x_o = x_o + dot(jnp.concatenate([real, imag], axis=0), u_h)
     x_h = complex_rows(x_h, PAD, PAD) + complex_rows(x_h_turned, PAD, DEEP)
     x_o = complex_rows(x_o, PAD, PAD) + complex_rows(x_o_turned, PAD, DEEP)
+
+    swap[1].wait_recv()
+    both, rest = arrived[1, :PAD], arrived[1, PAD:, :PAD]
+    x_o = x_o + combine(dot(both[:, :DEEP], u_h), dot(both, lowered[:WIDE]) + dot_tn(rest, lowered[WIDE:]))
+    turned = dot_tn(both, u_o[:PAD])
+    imag = jnp.concatenate([turned[ROWS:], dot(rest, u_o[:PAD])], axis=0)
+    x_h = x_h + jnp.concatenate([combine(turned[:ROWS], -imag), jnp.zeros((PAD - ROWS, COLS), F32)], axis=0)
 
     x_all = jnp.concatenate([x_h, x_o], axis=0)
     squares = jnp.sum(jnp.sum(x_all * x_all, axis=0, keepdims=True), axis=1, keepdims=True)
@@ -408,6 +415,7 @@
             pltpu.VMEM((2 * PAD, DEEP), F32),
             pltpu.VMEM((2, PAD + REST, WIDE), BF16),
             pltpu.VMEM((2, PAD + REST, WIDE), BF16),
+            pltpu.VMEM((2 * ROWS, COLS), BF16),
             pltpu.SemaphoreType.DMA,
             pltpu.SemaphoreType.DMA((SLOTS + GIFTS,)),
             pltpu.SemaphoreType.DMA,

time: 63.6 us -> 63.3 us (level)
  no operation moved by 1% of the time
where the time goes in v5:
time: 63.3 us; the launch traced here: 63.2 us
  Pallas kernels  60.7 us (96%)
  local copies, waits for them, and re-layouts  1.78 us (3%)
  between operations  0.66 us (1%)
    pallas_call x1, Pallas kernels, on_device(): pl.pallas_call(kernel, out_shape=jax.ShapeDtypeStruct((1, ROWS, COLS), F3...  60.7 us
    unnamed x1, local copies, waits for them, and re-layouts  1.78 us

profile of v5, /device:TPU:8, one launch (start us, length us, event | category | flops | bytes accessed | tf_op | source)
XLA Modules:
  0.0 63.2 jit_solution(2066845151852387710)
XLA Ops:
  0.7 60.7 %disentangle.1 = f32[1,200,512]{2,1,0:T(8,128)} custom-call(s32[1]{0:T(128)S(6)} %copy.6.window_ref, f32[12]{0:T(128)} %weight_ref.1, bf16[12,200,800]{2,1,0:T(8,128)(2,1)} %bitcast.1, bf16[1,200,512]{2,1,0:T(8,128)(2,1)} %own_ref.1), custom_call_target="tpu_custom_call" | custom-call | tf_op jit(solution)/shard_map/disentangle/pallas_call | solution.py:397
  61.4 1.8 %copy.7 = f32[1,200,512]{2,1,0:T(8,128)} copy(f32[1,200,512]{2,1,0:T(8,128)} %disentangle.1) | data formatting | bytes 819200
